TPU v7x, 8 devices: a whole 2x2x1 slice. The times are simulated.
8 devices in a mesh: dp: 2 (over y, z), tp: 4 (over x, core).
Axes of the slice: x: 2, y: 2, z: 1, core: 2. Of those that a mesh axis runs over, the one named last changes fastest.
Arguments:
- x: bfloat16 [128, 2048], P('dp'), parts along dimension 0
- k_cache: bfloat16 [128, 1024, 16, 128], P('dp', None, 'tp'), parts along dimension 0
- v_cache: bfloat16 [128, 1024, 16, 128], P('dp', None, 'tp'), parts along dimension 0
- gain_a: bfloat16 [2048], replicated
- wq: bfloat16 [2048, 2048], P(None, 'tp')
- wo: bfloat16 [2048, 2048], P('tp')
- gain_m: bfloat16 [2048], replicated
- w_gate: bfloat16 [2048, 8192], P(None, 'tp')
- w_up: bfloat16 [2048, 8192], P(None, 'tp')
- w_down: bfloat16 [8192, 2048], P('tp')
Outputs:
- output: bfloat16 [128, 2048], P('dp'), parts along dimension 0
There are 2 independent parts. A program takes and returns all parts, laid end to end along the dimension named above; an argument that names none is the same for every part.
All inputs are finite; a program needn't handle non-finite values.
Results may differ from a plain program's by a relative error of at most 0.017.
Values are sent between devices in bfloat16 or wider.
A program may use at most 2 GiB of HBM per device.

v0:
```python
import jax
import jax.numpy as jnp
from jax import lax
from jax.sharding import PartitionSpec as P

HEAD = 128
THETA = 10000


def normed(x, gain):
    wide = x.astype(jnp.float32)
    scale = lax.rsqrt(jnp.mean(wide * wide, -1, keepdims=True) + 1e-6)
    return (wide * scale * gain.astype(jnp.float32)).astype(jnp.bfloat16)


def turned(t, place, theta):
    half = t.shape[-1] // 2
    angle = place.astype(jnp.float32)[:, None] * theta ** (-jnp.arange(half, dtype=jnp.float32) / half)
    cos, sin = jnp.cos(angle)[:, None], jnp.sin(angle)[:, None]
    a, b = t[..., :half].astype(jnp.float32), t[..., half:].astype(jnp.float32)
    return jnp.concatenate([a * cos - b * sin, b * cos + a * sin], -1).astype(jnp.bfloat16)


def matmul(a, w):
    return jnp.dot(a, w, preferred_element_type=jnp.float32).astype(jnp.bfloat16)


def einsum(form, a, b):
    return jnp.einsum(form, a.astype(jnp.float32), b.astype(jnp.float32))


def seen_by(a, wq, k_cache, v_cache, head, theta):
    batch, cache, kv_heads = k_cache.shape[:3]
    place = jnp.full((batch,), cache - 1)
    q = turned(matmul(a, wq).reshape(batch, -1, head), place, theta).reshape(batch, kv_heads, -1, head)
    scores = einsum("bgsd,bugd->bgsu", q, k_cache) * head**-0.5
    weights = jax.nn.softmax(scores, -1).astype(jnp.bfloat16)
    return einsum("bgsu,bugd->bgsd", weights, v_cache).astype(jnp.bfloat16).reshape(batch, -1)


def hidden_of(b, w_gate, w_up):
    gate = jnp.dot(b, w_gate, preferred_element_type=jnp.float32)
    up = jnp.dot(b, w_up, preferred_element_type=jnp.float32)
    return (jax.nn.silu(gate) * up).astype(jnp.bfloat16)


def solution(mesh):
    def added(t, term):
        return (t.astype(jnp.float32) + lax.psum(term.astype(jnp.bfloat16), "tp").astype(jnp.float32)).astype(jnp.bfloat16)

    def step(x, k_cache, v_cache, gain_a, wq, wo, gain_m, w_gate, w_up, w_down):
        seen = seen_by(normed(x, gain_a), wq, k_cache, v_cache, HEAD, THETA)
        h = added(x, jnp.dot(seen, wo, preferred_element_type=jnp.float32))
        return added(h, jnp.dot(hidden_of(normed(h, gain_m), w_gate, w_up), w_down, preferred_element_type=jnp.float32))

    states, cache, columns, rows_of = P("dp", None), P("dp", None, "tp", None), P(None, "tp"), P("tp", None)
    return jax.shard_map(
        step,
        mesh=mesh,
        in_specs=(states, cache, cache, P(None), columns, rows_of, P(None), columns, columns, rows_of),
        out_specs=states,
        check_vma=False,
    )
```

profile of v0, /device:TPU:0, one launch (start us, length us, event | category | flops | bytes accessed | tf_op | source)
XLA Modules:
  0.0 151.5 jit_solution(449007839502723109)
XLA Ops:
  6.5 0.0 copy-start
  6.5 0.0 all-reduce.3.cloned.1.call-start
  6.6 0.8 convert_element_type.66
  7.4 1.1 fusion.14
  8.5 2.2 %convolution_convert_fusion.2 = bf16[64,512]{1,0:T(8,128)(2,1)S(1)} fusion(bf16[2048,512]{1,0:T(8,128)(2,1)} %param.14, bf16[64,2048]{1,0:T(8,128)(2,1)} %param.10, f32[2048]{0:T(1024)S(1)} %convert_element_type.66, f32[64]{0:T(128)S(1)} %add_rsqrt_fusion.1), kind=kOutput, calls=%fused_computation.15 | convolution fusion | flops 134774784 | bytes 2433280 | tf_op jit(solution)/shard_map/dot_general | solution.py:25
  10.8 0.1 fusion.51
  11.0 0.1 maximum_bitcast_fusion
  11.1 30.6 %fusion.4 = f32[64,4,1,1024]{3,2,1,0:T(1,128)S(1)} fusion(bf16[64,1024,4,128]{3,2,1,0:T(4,128)(2,1)} %param.11, bf16[64,4,128,1]{2,0,1,3:T(8,128)(2,1)S(1)} %maximum_bitcast_fusion), kind=kOutput, calls=%fused_computation.4 | convolution fusion | flops 67108864 | bytes 68222976 | tf_op jit(solution)/shard_map/bgsd,bugd->bgsu/dot_general | solution.py:29
  41.7 2.2 %fusion.11 = bf16[64,4,1024,1]{2,0,1,3:T(8,128)(2,1)} fusion(f32[64,4,1,1024]{3,2,1,0:T(1,128)S(1)} %fusion.4), kind=kOutput, calls=%fused_computation.14 | output fusion | flops 1051134 | bytes 1572864 | tf_op jit(solution)/shard_map/div | solution.py:37
  43.9 0.0 copy-start.2
  43.9 0.0 copy-start.1
  43.9 25.7 %fusion.2 = f32[64,4,1,128]{3,2,1,0:T(1,128)S(1)} fusion(bf16[64,1024,4,128]{3,2,1,0:T(4,128)(2,1)} %param.12, bf16[64,4,1024,1]{2,0,1,3:T(8,128)(2,1)} %fusion.11), kind=kOutput, calls=%fused_computation.2 | convolution fusion | flops 67108864 | bytes 67764224 | tf_op jit(solution)/shard_map/bgsu,bugd->bgsd/dot_general | solution.py:29
  69.6 0.0 copy-done
  69.6 1.2 convolution_convert_fusion.1
  70.8 0.0 all-reduce.3.cloned.1.call-update
  70.8 0.2 all-reduce.5.cloned.1.call-start
  71.1 0.0 copy-done.2
  71.1 29.3 %all-reduce.3.cloned.1.call-done = bf16[64,2048]{1,0:T(8,128)(2,1)} async-done(((bf16[64,2048]{1,0:T(8,128)(2,1)}), bf16[64,2048]{1,0:T(8,128)(2,1)}) %all-reduce.3.cloned.1.call-update) | async-done | bytes 262160 | tf_op jit(solution)/shard_map/psum | solution.py:49
  100.4 0.0 copy-done.1
  100.4 1.1 fusion.18
  101.6 5.0 %fusion.39 = f32[64,2048]{1,0:T(8,128)S(1)} fusion(bf16[2048,2048]{1,0:T(8,128)(2,1)} %param.17, bf16[64,2048]{1,0:T(8,128)(2,1)S(1)} %get-tuple-element.6, f32[2048]{0:T(1024)S(1)} %convert_element_type.77, f32[64]{0:T(128)S(1)} %add_rsqrt_fusion), kind=kOutput, calls=%fused_computation.51 | convolution fusion | flops 537395200 | bytes 9183488 | tf_op jit(solution)/shard_map/dot_general | solution.py:42
  106.6 9.5 %convolution_convert_fusion = bf16[64,2048]{1,0:T(8,128)(2,1)} fusion(bf16[2048,2048]{1,0:T(8,128)(2,1)} %param.19, bf16[2048,2048]{1,0:T(8,128)(2,1)} %param.18, f32[64,2048]{1,0:T(8,128)S(1)} %fusion.39, bf16[64,2048]{1,0:T(8,128)(2,1)S(1)} %get-tuple-element.6, f32[2048]{0:T(1024)S(1)} %convert_element_type.77, f32[64]{0:T(128)S(1)} %add_rsqrt_fusion), kind=kOutput, calls=%fused_computation.8 | convolution fusion | flops 1075183616 | bytes 17834240 | tf_op jit(solution)/shard_map/dot_general | solution.py:54
  116.1 0.0 all-reduce.5.cloned.1.call-update
  116.2 26.8 %all-reduce.5.cloned.1.call-done = bf16[64,2048]{1,0:T(8,128)(2,1)} async-done(((bf16[64,2048]{1,0:T(8,128)(2,1)}), bf16[64,2048]{1,0:T(8,128)(2,1)}) %all-reduce.5.cloned.1.call-update) | async-done | bytes 262160 | tf_op jit(solution)/shard_map/psum | solution.py:49
  142.9 1.7 %fusion.21 = bf16[64,2048]{1,0:T(8,128)(2,1)} fusion(bf16[64,2048]{1,0:T(8,128)(2,1)S(1)} %get-tuple-element.6, bf16[64,2048]{1,0:T(8,128)(2,1)} %all-reduce.5.cloned.1.call-done), kind=kLoop, calls=%fused_computation.32 | loop fusion | flops 524288 | bytes 786432 | tf_op jit(solution)/shard_map/convert_element_type | solution.py:49
  (7 shorter events, 0.2 us)
Async XLA Ops:
  6.5 63.1 %copy-start = (bf16[512,2048]{1,0:T(8,128)(2,1)S(1)}, bf16[512,2048]{1,0:T(8,128)(2,1)}, u32[]{:S(2)}) copy-start(bf16[512,2048]{1,0:T(8,128)(2,1)} %param.15) | copy-start | bytes 6291460
  6.5 93.9 %all-reduce.3.cloned.1.call-start = ((), (), s32[]{:S(2)}) async-start(), calls=%async_computation | async-start | bytes 524288 | tf_op jit(solution)/shard_map/psum | solution.py:49
  43.9 27.2 %copy-start.2 = (bf16[2048]{0:T(1024)(128)(2,1)S(1)}, bf16[2048]{0:T(1024)(128)(2,1)}, u32[]{:S(2)}) copy-start(bf16[2048]{0:T(1024)(128)(2,1)} %param.16) | copy-start | bytes 12292
  43.9 56.5 %copy-start.1 = (bf16[64,2048]{1,0:T(8,128)(2,1)S(1)}, bf16[64,2048]{1,0:T(8,128)(2,1)}, u32[]{:S(2)}) copy-start(bf16[64,2048]{1,0:T(8,128)(2,1)} %param.10) | copy-start | bytes 786436
  70.8 72.1 %all-reduce.5.cloned.1.call-start = ((), (), s32[]{:S(2)}) async-start(), calls=%async_computation.1 | async-start | bytes 524288 | tf_op jit(solution)/shard_map/psum | solution.py:49
Sparse Core Ops, SparseCore 0:
  71.0 29.4 all-reduce.2
  116.3 26.5 all-reduce.4
where the time goes:
time: 152 us; the launch traced here: 151 us
  matrix products  74.3 us (49%)
  waiting for transfers between devices  56.1 us (37%)
  between operations  13.5 us (9%)
  other arithmetic  7.24 us (5%)
    dot_general x2, matrix products, einsum(): return jnp.einsum(form, a.astype(jnp.float32), b.astype(jnp.float32))  56.3 us
    psum x2, waiting for transfers between devices, added(): lax.psum(term.astype(jnp.bfloat16), 'tp').astype(jnp.float32)  56.1 us
    dot_general x1, matrix products, step(): jnp.dot(hidden_of(normed(h, gain_m), w_gate, w_up), w_down, preferred_ele...  9.54 us
    dot_general x1, matrix products, hidden_of(): gate = jnp.dot(b, w_gate, preferred_element_type=jnp.float32)  5.01 us
  transfers between devices with their start and end apart: 2, of which 2 were waited for; matrix products, arithmetic and copies ran while one was open for 0% of the time, Pallas kernels for 0%

commit v1 on v0

v1 whole, which is shorter than its diff:
```python
import jax
import jax.numpy as jnp
import numpy as np
from jax import lax
from jax.experimental import pallas as pl
from jax.experimental.pallas import tpu as pltpu
from jax.sharding import PartitionSpec as P

MESH = pl.DeviceIdType.MESH
HEAD = 128
THETA = 10000
ROWS, D, CACHE, HEADS = 64, 2048, 1024, 4
KV = CACHE * HEADS
PAIRS = ROWS // 2
DEPTH = 6
CHUNK = 16
CHUNKS = ROWS // CHUNK
PER = CHUNK // 2
HALF = D // 2
FF = 2048
NCOL = 512
PIECES = D // NCOL
F32, BF16 = jnp.float32, jnp.bfloat16


def dot(a, b):
    return jnp.dot(a, b, preferred_element_type=F32)


def rope_table():
    half = HEAD // 2
    angle = np.float32(CACHE - 1) * np.float32(THETA) ** (-np.arange(half, dtype=np.float32) / np.float32(half))
    cos, sin = np.cos(angle), np.sin(angle)
    table = np.zeros((8, HEAD), np.float32)
    table[0] = np.concatenate([cos, cos])
    table[1] = np.concatenate([-sin, sin])
    return table


def normed(parts, gain):
    total = parts[0] * parts[0]
    for p in parts[1:]:
        total = total + p * p
    scale = lax.rsqrt(jnp.sum(total, -1, keepdims=True) * (1.0 / D) + 1e-6)
    return [(p * scale * gain[j : j + 1]).astype(BF16) for j, p in enumerate(parts)]


def kernel(
    x_hbm, k_hbm, v_hbm, ga_hbm, wq_hbm, wo_hbm, gm_hbm, wg_hbm, wu_hbm, wd_hbm, rope_hbm, y_hbm,
    xb, ga, gm, rope, wq, wo, wm, kbuf, vbuf, q_s, w_s, o_s, act, hid,
    t1, r1, a1, b1, hb, t2, r2, a2, b2, yb,
    in_sem, k_sem, v_sem, wm_sem, s1, s2, y_sem,
):
    tp = lax.axis_index("tp")
    core = lax.rem(tp, 2)
    chip = tp // 2
    other = 1 - core
    mate = {"tp": chip * 2 + other}
    across = {"tp": (1 - chip) * 2 + core}

    barrier = pltpu.get_barrier_semaphore()
    for device in (mate, across):
        pl.semaphore_signal(barrier, inc=1, device_id=device, device_id_type=MESH)

    def k_copy(i):
        slot = lax.rem(i, DEPTH)
        return pltpu.make_async_copy(k_hbm.at[i // PER, :, lax.rem(i, PER)], kbuf.at[slot], k_sem.at[slot])

    def v_copy(i):
        slot = lax.rem(i, DEPTH)
        return pltpu.make_async_copy(v_hbm.at[i // PER, :, lax.rem(i, PER)], vbuf.at[slot], v_sem.at[slot])

    def wm_copy(w_hbm, n, piece):
        cols = pl.ds(pl.multiple_of(n * NCOL, NCOL), NCOL)
        return pltpu.make_async_copy(w_hbm.at[:, cols], wm.at[piece], wm_sem.at[piece])

    firsts = [
        pltpu.make_async_copy(src, dst, in_sem.at[n])
        for n, (src, dst) in enumerate([(x_hbm, xb), (ga_hbm, ga), (rope_hbm, rope), (wq_hbm, wq), (gm_hbm, gm)])
    ]
    wo_copy = pltpu.make_async_copy(wo_hbm, wo, in_sem.at[5])
    for c in firsts:
        c.start()

    @pl.loop(0, DEPTH)
    def _(i):
        k_copy(i).start()
        v_copy(i).start()

    for c in firsts:
        c.wait()
    blocks = [xb[:, j * 128 : (j + 1) * 128].astype(F32) for j in range(D // 128)]
    for j, b in enumerate(normed(blocks, ga[...].astype(F32))):
        act[:, j * 128 : (j + 1) * 128] = b
    q = dot(act[...], wq[...]).astype(BF16).astype(F32)
    cos, sin = rope[0:1, :], rope[1:2, :]
    for h in range(HEADS):
        t = q[:, h * HEAD : (h + 1) * HEAD]
        t = t * cos + pltpu.roll(t, HEAD // 2, 1) * sin
        q_s[:, h * HEAD : (h + 1) * HEAD] = t.astype(BF16).astype(F32)

    row = lax.broadcasted_iota(jnp.int32, (8, HEAD), 0)

    def scores(i):
        slot = lax.rem(i, DEPTH)
        halves = []
        for s in range(2):
            one = q_s[pl.ds(i // PER * CHUNK + s * PER + lax.rem(i, PER), 1), :]
            lhs = jnp.zeros((8, HEAD), F32)
            for h in range(HEADS):
                lhs = jnp.where(row == 4 * s + h, one[:, h * HEAD : (h + 1) * HEAD], lhs)
            halves.append(lhs)
        lhs = jnp.concatenate(halves, 1).astype(BF16)
        keys = jnp.concatenate([kbuf[slot, 0], kbuf[slot, 1]], 1)
        sc = lax.dot_general(lhs, keys, (((1,), (1,)), ((), ())), preferred_element_type=F32)
        r = lax.broadcasted_iota(jnp.int32, (8, KV), 0)
        c = lax.broadcasted_iota(jnp.int32, (8, KV), 1)
        sc = jnp.where(jnp.bitwise_and(r, 3) == jnp.bitwise_and(c, 3), sc * HEAD**-0.5, -jnp.inf)
        e = jnp.exp(sc - jnp.max(sc, -1, keepdims=True))
        w_s[...] = (e * (1.0 / jnp.sum(e, -1, keepdims=True))).astype(BF16)

    def values(i):
        slot = lax.rem(i, DEPTH)
        vals = jnp.concatenate([vbuf[slot, 0], vbuf[slot, 1]], 1)
        return dot(w_s[...], vals)

    def send(src, dst, sems, n, device):
        return pltpu.make_async_remote_copy(
            src_ref=src, dst_ref=dst, send_sem=sems.at[0, n], recv_sem=sems.at[1, n], device_id=device, device_id_type=MESH
        )

    def first_a(j):
        return send(t1.at[j, other], r1.at[j], s1.at[0], j, mate)

    def first_b(j):
        return send(a1.at[j], b1.at[j], s1.at[1], j, across)

    def first_c(j):
        return send(hb.at[core, j], hb.at[core, j], s1.at[2], j, mate)

    def project(j):
        o = jnp.concatenate(
            [
                jnp.concatenate([o_s[pl.ds(j * PER, PER), 4 * s + h, s * HEAD : (s + 1) * HEAD] for h in range(HEADS)], 1)
                for s in range(2)
            ],
            0,
        ).astype(BF16)
        for s in range(2):
            t1[j, s] = dot(o, wo[:, s * HALF : (s + 1) * HALF]).astype(BF16)
        first_a(j).start()

    def fold(j):
        first_a(j).wait()
        a1[j] = (t1[j, core].astype(F32) + r1[j].astype(F32)).astype(BF16)
        first_b(j).start()

    def finish(j):
        first_b(j).wait()
        mine = xb[pl.ds(pl.multiple_of(j * CHUNK, CHUNK), CHUNK), pl.ds(pl.multiple_of(core * HALF, HALF), HALF)].astype(F32)
        hb[core, j] = (mine + (a1[j].astype(F32) + b1[j].astype(F32))).astype(BF16)
        first_c(j).start()

    k_copy(0).wait()
    scores(0)
    k_copy(DEPTH).start()

    @pl.loop(1, PAIRS)
    def _(i):
        k_copy(i).wait()
        v_copy(i - 1).wait()
        out = values(i - 1)
        scores(i)
        o_s[i - 1] = out

        @pl.when(i + DEPTH < PAIRS)
        def _():
            k_copy(i + DEPTH).start()

        @pl.when(i - 1 + DEPTH < PAIRS)
        def _():
            v_copy(i - 1 + DEPTH).start()

        @pl.when(i == 3)
        def _():
            wo_copy.start()

        n = i - 1 + DEPTH - PAIRS

        @pl.when((n >= 0) & (n < PIECES))
        def _():
            wm_copy(wg_hbm, n, n).start()
            wm_copy(wu_hbm, n, PIECES + n).start()

        @pl.when(n == PIECES)
        def _():
            wm_copy(wd_hbm, 0, 2 * PIECES).start()
            wm_copy(wd_hbm, 1, 2 * PIECES + 1).start()

        j = i // PER - 1
        step = lax.rem(i, PER)

        @pl.when(i == PER)
        def _():
            wo_copy.wait()
            pl.semaphore_wait(barrier, 2)

        @pl.when((i >= PER) & (step == 0))
        def _():
            project(j)

        @pl.when((i >= PER) & (step == 2))
        def _():
            fold(j)

        @pl.when((i >= PER) & (step == 5))
        def _():
            finish(j)

    wm_copy(wd_hbm, 2, 2 * PIECES + 2).start()
    wm_copy(wd_hbm, 3, 2 * PIECES + 3).start()
    v_copy(PAIRS - 1).wait()
    o_s[PAIRS - 1] = values(PAIRS - 1)
    last = CHUNKS - 1
    project(last)
    fold(last)
    finish(last)
    for j in range(CHUNKS):
        first_c(j).wait()

    h = [hb[s].reshape(ROWS, HALF) for s in range(2)]
    blocks = [h[j // 8][:, (j % 8) * 128 : (j % 8 + 1) * 128].astype(F32) for j in range(D // 128)]
    for j, b in enumerate(normed(blocks, gm[...].astype(F32))):
        act[:, j * 128 : (j + 1) * 128] = b

    @pl.loop(0, PIECES)
    def _(n):
        wm_copy(wg_hbm, n, n).wait()
        wm_copy(wu_hbm, n, PIECES + n).wait()
        gate = dot(act[...], wm[n])
        up = dot(act[...], wm[PIECES + n])
        hid[n] = (gate * (1.0 / (1.0 + jnp.exp(-gate))) * up).astype(BF16)

    def second_a(n):
        return send(t2.at[n, other], r2.at[n], s2.at[0], n, mate)

    def second_b(n):
        return send(a2.at[n], b2.at[n], s2.at[1], n, across)

    def cols_of(n):
        return pl.ds(pl.multiple_of(n * NCOL + core * (NCOL // 2), NCOL // 2), NCOL // 2)

    def second_c(n):
        return send(yb.at[n], y_hbm.at[:, cols_of(n)], s2.at[2], n, mate)

    def y_copy(n):
        return pltpu.make_async_copy(yb.at[n], y_hbm.at[:, cols_of(n)], y_sem.at[n])

    @pl.loop(0, PIECES)
    def _(n):
        wm_copy(wd_hbm, n, 2 * PIECES + n).wait()
        t = dot(hid[0], wm[2 * PIECES + n, 0:NCOL])
        for m in range(1, PIECES):
            t = t + dot(hid[m], wm[2 * PIECES + n, m * NCOL : (m + 1) * NCOL])
        for s in range(2):
            t2[n, s] = t[:, s * (NCOL // 2) : (s + 1) * (NCOL // 2)].astype(BF16)
        second_a(n).start()

    @pl.loop(0, PIECES)
    def _(n):
        second_a(n).wait()
        a2[n] = (t2[n, core].astype(F32) + r2[n].astype(F32)).astype(BF16)
        second_b(n).start()

    @pl.loop(0, PIECES)
    def _(n):
        second_b(n).wait()
        off = pl.multiple_of(lax.rem(n, 2) * NCOL + core * (NCOL // 2), NCOL // 2)
        mine = hb[n // 2, :, :, pl.ds(off, NCOL // 2)].reshape(ROWS, NCOL // 2).astype(F32)
        yb[n] = (mine + (a2[n].astype(F32) + b2[n].astype(F32))).astype(BF16)
        second_c(n).start()
        y_copy(n).start()

    @pl.loop(0, PIECES)
    def _(n):
        second_c(n).wait()
        y_copy(n).wait()


def layer(x, k_cache, v_cache, gain_a, wq, wo, gain_m, w_gate, w_up, w_down):
    hbm = pl.BlockSpec(memory_space=pl.ANY)
    vmem, dma = pltpu.VMEM, pltpu.SemaphoreType.DMA
    return pl.pallas_call(
        kernel,
        out_shape=jax.ShapeDtypeStruct((ROWS, D), BF16),
        in_specs=[hbm] * 11,
        out_specs=hbm,
        scratch_shapes=[
            vmem((ROWS, D), BF16),
            vmem((D // 128, 128), BF16),
            vmem((D // 128, 128), BF16),
            vmem((8, HEAD), F32),
            vmem((D, HEADS * HEAD), BF16),
            vmem((HEADS * HEAD, D), BF16),
            vmem((3 * PIECES, D, NCOL), BF16),
            vmem((DEPTH, 2, KV, HEAD), BF16),
            vmem((DEPTH, 2, KV, HEAD), BF16),
            vmem((ROWS, HEADS * HEAD), F32),
            vmem((8, KV), BF16),
            vmem((PAIRS, 8, 2 * HEAD), F32),
            vmem((ROWS, D), BF16),
            vmem((PIECES, ROWS, NCOL), BF16),
            vmem((CHUNKS, 2, CHUNK, HALF), BF16),
            vmem((CHUNKS, CHUNK, HALF), BF16),
            vmem((CHUNKS, CHUNK, HALF), BF16),
            vmem((CHUNKS, CHUNK, HALF), BF16),
            vmem((2, CHUNKS, CHUNK, HALF), BF16),
            vmem((PIECES, 2, ROWS, NCOL // 2), BF16),
            vmem((PIECES, ROWS, NCOL // 2), BF16),
            vmem((PIECES, ROWS, NCOL // 2), BF16),
            vmem((PIECES, ROWS, NCOL // 2), BF16),
            vmem((PIECES, ROWS, NCOL // 2), BF16),
            dma((6,)),
            dma((DEPTH,)),
            dma((DEPTH,)),
            dma((3 * PIECES,)),
            dma((3, 2, CHUNKS)),
            dma((3, 2, PIECES)),
            dma((PIECES,)),
        ],
        compiler_params=pltpu.CompilerParams(collective_id=0, has_side_effects=True, vmem_limit_bytes=67043328),
    )(
        x,
        k_cache.reshape(CHUNKS, 2, PER, KV, HEAD),
        v_cache.reshape(CHUNKS, 2, PER, KV, HEAD),
        gain_a.reshape(D // 128, 128),
        wq,
        wo,
        gain_m.reshape(D // 128, 128),
        w_gate,
        w_up,
        w_down,
        jnp.asarray(rope_table()),
    )


def solution(mesh):
    states, cache, columns, rows_of = P("dp", None), P("dp", None, "tp", None), P(None, "tp"), P("tp", None)
    return jax.shard_map(
        layer,
        mesh=mesh,
        in_specs=(states, cache, cache, P(None), columns, rows_of, P(None), columns, columns, rows_of),
        out_specs=states,
        check_vma=False,
    )
```

time: 152 us -> 63.9 us (0.42)
  matrix products: 74.3 us -> 0 us
  Pallas kernels: 0 us -> 62.1 us
  waiting for transfers between devices: 56.1 us -> 0 us
  between operations: 13.5 us -> 0.01 us
  other arithmetic: 7.24 us -> 0 us
  local copies, waits for them, and re-layouts: 0.14 us -> 1.67 us
    dot_general x6 -> x0, matrix products: 74.3 us -> none  [the longest x2 56.3 us: einsum(): return jnp.einsum(form, a.astype(jnp.float32), b.astype(jnp.float32))]
    pallas_call x0 -> x1, Pallas kernels: none -> 62.1 us  [layer(): pl.pallas_call(kernel, out_shape=jax.ShapeDtypeStruct((ROWS, D), BF16), i...]
    psum x2 -> x0, waiting for transfers between devices: 56.1 us -> none  [added(): lax.psum(term.astype(jnp.bfloat16), 'tp').astype(jnp.float32)]
    convert_element_type x4 -> x0, other arithmetic: 2.57 us -> none  [the longest x1 1.71 us: added(): (t.astype(jnp.float32) + lax.psum(term.astype(jnp.bfloat16), 'tp').astype...]
    reduce_sum x2 -> x0, other arithmetic: 2.24 us -> none  [normed(): scale = lax.rsqrt(jnp.mean(wide * wide, -1, keepdims=True) + 1e-06)]
    div x1 -> x0, other arithmetic: 2.22 us -> none  [seen_by(): weights = jax.nn.softmax(scores, -1).astype(jnp.bfloat16)]
    unnamed x6 -> x1, local copies, waits for them, and re-layouts: 0.01 us -> 1.67 us
  transfers between devices with their start and end apart: 2 -> 0, of which waited for: 2 -> 0; matrix products, arithmetic and copies ran while one was open for 0% -> 0% of each run, Pallas kernels for 0% -> 0%
where the time goes in v1:
time: 63.9 us; the launch traced here: 63.8 us
  Pallas kernels  62.1 us (97%)
  local copies, waits for them, and re-layouts  1.67 us (3%)
    pallas_call x1, Pallas kernels, layer(): pl.pallas_call(kernel, out_shape=jax.ShapeDtypeStruct((ROWS, D), BF16), i...  62.1 us
    unnamed x1, local copies, waits for them, and re-layouts  1.67 us

profile of v1, /device:TPU:0, one launch (start us, length us, event | category | flops | bytes accessed | tf_op | source)
XLA Modules:
  0.0 63.8 jit_solution(3174245959781730023)
XLA Ops:
  0.0 62.1 %shard_map.109 = bf16[64,2048]{1,0:T(8,128)(2,1)} custom-call(bf16[64,2048]{1,0:T(8,128)(2,1)} %x_hbm.1, bf16[4,2,8,4096,128]{4,3,2,1,0:T(8,128)(2,1)} %bitcast.k_hbm, bf16[4,2,8,4096,128]{4,3,2,1,0:T(8,128)(2,1)} %bitcast.1.v_hbm, bf16[16,128]{1,0:T(8,128)(2,1)} %bitcast.4, bf16[2048,512]{1,0:T(8,128)(2,1)} %wq_hbm.1, bf16[512,2048]{1,0:T(8,128)(2,1)} %wo_hbm.1, ...), custom_call_target="tpu_custom_call" | custom-call | tf_op jit(solution)/shard_map/pallas_call | solution.py:293
  62.1 1.7 %copy.13 = bf16[64,2048]{1,0:T(8,128)(2,1)} copy(bf16[64,2048]{1,0:T(8,128)(2,1)} %shard_map.109) | data formatting | bytes 524288

commit v2 on v1

--- a/solution.py
+++ b/solution.py
@@ -13,7 +13,7 @@
 KV = CACHE * HEADS
 PAIRS = ROWS // 2
 DEPTH = 6
-CHUNK = 16
+CHUNK = 8
 CHUNKS = ROWS // CHUNK
 PER = CHUNK // 2
 HALF = D // 2
@@ -46,10 +46,10 @@
 
 
 def kernel(
-    x_hbm, k_hbm, v_hbm, ga_hbm, wq_hbm, wo_hbm, gm_hbm, wg_hbm, wu_hbm, wd_hbm, rope_hbm, y_hbm,
-    xb, ga, gm, rope, wq, wo, wm, kbuf, vbuf, q_s, w_s, o_s, act, hid,
-    t1, r1, a1, b1, hb, t2, r2, a2, b2, yb,
-    in_sem, k_sem, v_sem, wm_sem, s1, s2, y_sem,
+    x_hbm, k_hbm, v_hbm, ga_hbm, wq_hbm, wo_hbm, gm_hbm, wg_hbm, wu_hbm, wd_hbm, rope_hbm, y,
+    xb, ga, gm, rope, wq, wo, wm, kbuf, vbuf, q_s, s_s, o_s, act, hid,
+    t1, r1, a1, b1, hb, d1, t2, r2, a2, b2,
+    in_sem, k_sem, v_sem, wm_sem, s1, sd, s2,
 ):
     tp = lax.axis_index("tp")
     core = lax.rem(tp, 2)
@@ -57,9 +57,10 @@
     other = 1 - core
     mate = {"tp": chip * 2 + other}
     across = {"tp": (1 - chip) * 2 + core}
+    corner = {"tp": (1 - chip) * 2 + other}
 
     barrier = pltpu.get_barrier_semaphore()
-    for device in (mate, across):
+    for device in (mate, across, corner):
         pl.semaphore_signal(barrier, inc=1, device_id=device, device_id_type=MESH)
 
     def k_copy(i):
@@ -89,7 +90,7 @@
 
     for c in firsts:
         c.wait()
-    blocks = [xb[:, j * 128 : (j + 1) * 128].astype(F32) for j in range(D // 128)]
+    blocks = [xb[:, :, j * 128 : (j + 1) * 128].astype(F32).reshape(ROWS, 128) for j in range(D // 128)]
     for j, b in enumerate(normed(blocks, ga[...].astype(F32))):
         act[:, j * 128 : (j + 1) * 128] = b
     q = dot(act[...], wq[...]).astype(BF16).astype(F32)
@@ -112,17 +113,19 @@
             halves.append(lhs)
         lhs = jnp.concatenate(halves, 1).astype(BF16)
         keys = jnp.concatenate([kbuf[slot, 0], kbuf[slot, 1]], 1)
-        sc = lax.dot_general(lhs, keys, (((1,), (1,)), ((), ())), preferred_element_type=F32)
+        return lax.dot_general(lhs, keys, (((1,), (1,)), ((), ())), preferred_element_type=F32)
+
+    def weights(sc):
         r = lax.broadcasted_iota(jnp.int32, (8, KV), 0)
         c = lax.broadcasted_iota(jnp.int32, (8, KV), 1)
         sc = jnp.where(jnp.bitwise_and(r, 3) == jnp.bitwise_and(c, 3), sc * HEAD**-0.5, -jnp.inf)
         e = jnp.exp(sc - jnp.max(sc, -1, keepdims=True))
-        w_s[...] = (e * (1.0 / jnp.sum(e, -1, keepdims=True))).astype(BF16)
-
-    def values(i):
+        return (e * (1.0 / jnp.sum(e, -1, keepdims=True))).astype(BF16)
+
+    def values(i, w):
         slot = lax.rem(i, DEPTH)
         vals = jnp.concatenate([vbuf[slot, 0], vbuf[slot, 1]], 1)
-        return dot(w_s[...], vals)
+        return dot(w, vals)
 
     def send(src, dst, sems, n, device):
         return pltpu.make_async_remote_copy(
@@ -137,6 +140,9 @@
 
     def first_c(j):
         return send(hb.at[core, j], hb.at[core, j], s1.at[2], j, mate)
+
+    def direct(n):
+        return send(t1.at[CHUNKS - 1], d1.at[n], sd, n, (mate, across, corner)[n])
 
     def project(j):
         o = jnp.concatenate(
@@ -148,7 +154,6 @@
         ).astype(BF16)
         for s in range(2):
             t1[j, s] = dot(o, wo[:, s * HALF : (s + 1) * HALF]).astype(BF16)
-        first_a(j).start()
 
     def fold(j):
         first_a(j).wait()
@@ -157,21 +162,22 @@
 
     def finish(j):
         first_b(j).wait()
-        mine = xb[pl.ds(pl.multiple_of(j * CHUNK, CHUNK), CHUNK), pl.ds(pl.multiple_of(core * HALF, HALF), HALF)].astype(F32)
+        mine = xb[j, :, pl.ds(pl.multiple_of(core * HALF, HALF), HALF)].astype(F32)
         hb[core, j] = (mine + (a1[j].astype(F32) + b1[j].astype(F32))).astype(BF16)
         first_c(j).start()
 
     k_copy(0).wait()
-    scores(0)
+    s_s[...] = scores(0)
     k_copy(DEPTH).start()
 
     @pl.loop(1, PAIRS)
     def _(i):
         k_copy(i).wait()
         v_copy(i - 1).wait()
-        out = values(i - 1)
-        scores(i)
-        o_s[i - 1] = out
+        w = weights(s_s[...])
+        sc = scores(i)
+        o_s[i - 1] = values(i - 1, w)
+        s_s[...] = sc
 
         @pl.when(i + DEPTH < PAIRS)
         def _():
@@ -203,43 +209,53 @@
         @pl.when(i == PER)
         def _():
             wo_copy.wait()
-            pl.semaphore_wait(barrier, 2)
+            pl.semaphore_wait(barrier, 3)
 
         @pl.when((i >= PER) & (step == 0))
         def _():
             project(j)
+            first_a(j).start()
 
         @pl.when((i >= PER) & (step == 2))
         def _():
             fold(j)
 
-        @pl.when((i >= PER) & (step == 5))
-        def _():
-            finish(j)
+        @pl.when((i >= 2 * PER) & (step == 3))
+        def _():
+            finish(j - 1)
 
     wm_copy(wd_hbm, 2, 2 * PIECES + 2).start()
     wm_copy(wd_hbm, 3, 2 * PIECES + 3).start()
+    w = weights(s_s[...])
     v_copy(PAIRS - 1).wait()
-    o_s[PAIRS - 1] = values(PAIRS - 1)
+    o_s[PAIRS - 1] = values(PAIRS - 1, w)
     last = CHUNKS - 1
     project(last)
-    fold(last)
-    finish(last)
-    for j in range(CHUNKS):
+    for n in range(3):
+        direct(n).start()
+    finish(last - 1)
+    for j in range(last):
         first_c(j).wait()
-
-    h = [hb[s].reshape(ROWS, HALF) for s in range(2)]
-    blocks = [h[j // 8][:, (j % 8) * 128 : (j % 8 + 1) * 128].astype(F32) for j in range(D // 128)]
+    for n in range(3):
+        direct(n).wait()
+    for s in range(2):
+        near = t1[last, s].astype(F32) + d1[0, s].astype(F32)
+        far = d1[1, s].astype(F32) + d1[2, s].astype(F32)
+        hb[s, last] = (xb[last, :, s * HALF : (s + 1) * HALF].astype(F32) + (near + far)).astype(BF16)
+
+    h = [hb[s].astype(F32).reshape(ROWS, HALF) for s in range(2)]
+    blocks = [h[j // 8][:, (j % 8) * 128 : (j % 8 + 1) * 128] for j in range(D // 128)]
     for j, b in enumerate(normed(blocks, gm[...].astype(F32))):
         act[:, j * 128 : (j + 1) * 128] = b
 
-    @pl.loop(0, PIECES)
-    def _(n):
+    for n in range(PIECES):
         wm_copy(wg_hbm, n, n).wait()
         wm_copy(wu_hbm, n, PIECES + n).wait()
-        gate = dot(act[...], wm[n])
-        up = dot(act[...], wm[PIECES + n])
-        hid[n] = (gate * (1.0 / (1.0 + jnp.exp(-gate))) * up).astype(BF16)
+    for n in range(FF // 256):
+        cols = slice(n % 2 * 256, n % 2 * 256 + 256)
+        gate = dot(act[...], wm[n // 2, :, cols])
+        up = dot(act[...], wm[PIECES + n // 2, :, cols])
+        hid[:, n * 256 : (n + 1) * 256] = (gate * (1.0 / (1.0 + jnp.exp(-gate))) * up).astype(BF16)
 
     def second_a(n):
         return send(t2.at[n, other], r2.at[n], s2.at[0], n, mate)
@@ -251,40 +267,25 @@
         return pl.ds(pl.multiple_of(n * NCOL + core * (NCOL // 2), NCOL // 2), NCOL // 2)
 
     def second_c(n):
-        return send(yb.at[n], y_hbm.at[:, cols_of(n)], s2.at[2], n, mate)
-
-    def y_copy(n):
-        return pltpu.make_async_copy(yb.at[n], y_hbm.at[:, cols_of(n)], y_sem.at[n])
-
-    @pl.loop(0, PIECES)
-    def _(n):
+        return send(y.at[:, cols_of(n)], y.at[:, cols_of(n)], s2.at[2], n, mate)
+
+    for n in range(PIECES):
         wm_copy(wd_hbm, n, 2 * PIECES + n).wait()
-        t = dot(hid[0], wm[2 * PIECES + n, 0:NCOL])
-        for m in range(1, PIECES):
-            t = t + dot(hid[m], wm[2 * PIECES + n, m * NCOL : (m + 1) * NCOL])
         for s in range(2):
-            t2[n, s] = t[:, s * (NCOL // 2) : (s + 1) * (NCOL // 2)].astype(BF16)
+            t2[n, s] = dot(hid[...], wm[2 * PIECES + n, :, s * (NCOL // 2) : (s + 1) * (NCOL // 2)]).astype(BF16)
         second_a(n).start()
-
-    @pl.loop(0, PIECES)
-    def _(n):
+    for n in range(PIECES):
         second_a(n).wait()
         a2[n] = (t2[n, core].astype(F32) + r2[n].astype(F32)).astype(BF16)
         second_b(n).start()
-
-    @pl.loop(0, PIECES)
-    def _(n):
+    for n in range(PIECES):
         second_b(n).wait()
-        off = pl.multiple_of(lax.rem(n, 2) * NCOL + core * (NCOL // 2), NCOL // 2)
-        mine = hb[n // 2, :, :, pl.ds(off, NCOL // 2)].reshape(ROWS, NCOL // 2).astype(F32)
-        yb[n] = (mine + (a2[n].astype(F32) + b2[n].astype(F32))).astype(BF16)
+        off = pl.multiple_of(n % 2 * NCOL + core * (NCOL // 2), NCOL // 2)
+        mine = hb[n // 2, :, :, pl.ds(off, NCOL // 2)].astype(F32).reshape(ROWS, NCOL // 2)
+        y[:, cols_of(n)] = (mine + (a2[n].astype(F32) + b2[n].astype(F32))).astype(BF16)
         second_c(n).start()
-        y_copy(n).start()
-
-    @pl.loop(0, PIECES)
-    def _(n):
+    for n in range(PIECES):
         second_c(n).wait()
-        y_copy(n).wait()
 
 
 def layer(x, k_cache, v_cache, gain_a, wq, wo, gain_m, w_gate, w_up, w_down):
@@ -292,11 +293,11 @@
     vmem, dma = pltpu.VMEM, pltpu.SemaphoreType.DMA
     return pl.pallas_call(
         kernel,
-        out_shape=jax.ShapeDtypeStruct((ROWS, D), BF16),
+        out_shape=pltpu.VMEM((ROWS, D), BF16),
         in_specs=[hbm] * 11,
-        out_specs=hbm,
+        out_specs=pl.BlockSpec(memory_space=pltpu.VMEM),
         scratch_shapes=[
-            vmem((ROWS, D), BF16),
+            vmem((CHUNKS, CHUNK, D), BF16),
             vmem((D // 128, 128), BF16),
             vmem((D // 128, 128), BF16),
             vmem((8, HEAD), F32),
@@ -306,17 +307,17 @@
             vmem((DEPTH, 2, KV, HEAD), BF16),
             vmem((DEPTH, 2, KV, HEAD), BF16),
             vmem((ROWS, HEADS * HEAD), F32),
-            vmem((8, KV), BF16),
+            vmem((8, KV), F32),
             vmem((PAIRS, 8, 2 * HEAD), F32),
             vmem((ROWS, D), BF16),
-            vmem((PIECES, ROWS, NCOL), BF16),
+            vmem((ROWS, FF), BF16),
             vmem((CHUNKS, 2, CHUNK, HALF), BF16),
             vmem((CHUNKS, CHUNK, HALF), BF16),
             vmem((CHUNKS, CHUNK, HALF), BF16),
             vmem((CHUNKS, CHUNK, HALF), BF16),
             vmem((2, CHUNKS, CHUNK, HALF), BF16),
+            vmem((3, 2, CHUNK, HALF), BF16),
             vmem((PIECES, 2, ROWS, NCOL // 2), BF16),
-            vmem((PIECES, ROWS, NCOL // 2), BF16),
             vmem((PIECES, ROWS, NCOL // 2), BF16),
             vmem((PIECES, ROWS, NCOL // 2), BF16),
             vmem((PIECES, ROWS, NCOL // 2), BF16),
@@ -325,12 +326,12 @@
             dma((DEPTH,)),
             dma((3 * PIECES,)),
             dma((3, 2, CHUNKS)),
+            dma((2, 3)),
             dma((3, 2, PIECES)),
-            dma((PIECES,)),
         ],
-        compiler_params=pltpu.CompilerParams(collective_id=0, has_side_effects=True, vmem_limit_bytes=67043328),
+        compiler_params=pltpu.CompilerParams(collective_id=0, has_side_effects=True, vmem_limit_bytes=62000000),
     )(
-        x,
+        x.reshape(CHUNKS, CHUNK, D),
         k_cache.reshape(CHUNKS, 2, PER, KV, HEAD),
         v_cache.reshape(CHUNKS, 2, PER, KV, HEAD),
         gain_a.reshape(D // 128, 128),

time: 63.9 us -> 61.6 us (0.964)
  Pallas kernels: 62.1 us -> 60.8 us
  local copies, waits for them, and re-layouts: 1.67 us -> 0.71 us
    pallas_call x1, Pallas kernels: 62.1 us -> 60.8 us  [layer(): pl.pallas_call(kernel, out_shape=pltpu.VMEM((ROWS, D), BF16), in_specs=[h...]
    unnamed x1, local copies, waits for them, and re-layouts: 1.67 us -> 0.71 us
where the time goes in v2:
time: 61.6 us; the launch traced here: 61.5 us
  Pallas kernels  60.8 us (99%)
  local copies, waits for them, and re-layouts  0.71 us (1%)
    pallas_call x1, Pallas kernels, layer(): pl.pallas_call(kernel, out_shape=pltpu.VMEM((ROWS, D), BF16), in_specs=[h...  60.8 us

profile of v2, /device:TPU:0, one launch (start us, length us, event | category | flops | bytes accessed | tf_op | source)
XLA Modules:
  0.0 61.5 jit_solution(13897697735499057347)
XLA Ops:
  0.0 60.8 %shard_map.109 = bf16[64,2048]{1,0:T(8,128)(2,1)S(1)} custom-call(bf16[8,8,2048]{2,1,0:T(8,128)(2,1)} %bitcast.5, bf16[8,2,4,4096,128]{4,3,2,1,0:T(8,128)(2,1)} %bitcast.1.k_hbm, bf16[8,2,4,4096,128]{4,3,2,1,0:T(8,128)(2,1)} %bitcast.2.v_hbm, bf16[16,128]{1,0:T(8,128)(2,1)} %bitcast.6, bf16[2048,512]{1,0:T(8,128)(2,1)} %wq_hbm.1, bf16[512,2048]{1,0:T(8,128)(2,1)} %wo_hbm.1, ...), custom_call_target="tpu_custom_call" | custom-call | tf_op jit(solution)/shard_map/pallas_call | solution.py:294
  60.8 0.7 %copy.13 = bf16[64,2048]{1,0:T(8,128)(2,1)} copy(bf16[64,2048]{1,0:T(8,128)(2,1)S(1)} %shard_map.109) | data formatting | bytes 524288

commit v3 on v2

--- a/solution.py
+++ b/solution.py
@@ -20,6 +20,8 @@
 FF = 2048
 NCOL = 512
 PIECES = D // NCOL
+SUB = 256
+SUBS = HALF // SUB
 F32, BF16 = jnp.float32, jnp.bfloat16
 
 
@@ -72,7 +74,8 @@
         return pltpu.make_async_copy(v_hbm.at[i // PER, :, lax.rem(i, PER)], vbuf.at[slot], v_sem.at[slot])
 
     def wm_copy(w_hbm, n, piece):
-        cols = pl.ds(pl.multiple_of(n * NCOL, NCOL), NCOL)
+        start = n * NCOL if w_hbm is not wd_hbm else lax.rem(n // 2 + other, 2) * HALF + n % 2 * NCOL
+        cols = pl.ds(pl.multiple_of(start, NCOL), NCOL)
         return pltpu.make_async_copy(w_hbm.at[:, cols], wm.at[piece], wm_sem.at[piece])
 
     firsts = [
@@ -85,8 +88,8 @@
 
     @pl.loop(0, DEPTH)
     def _(i):
-        k_copy(i).start()
-        v_copy(i).start()
+        k_copy(i).start(priority=1)
+        v_copy(i).start(priority=1)
 
     for c in firsts:
         c.wait()
@@ -168,9 +171,9 @@
 
     k_copy(0).wait()
     s_s[...] = scores(0)
-    k_copy(DEPTH).start()
-
-    @pl.loop(1, PAIRS)
+    k_copy(DEPTH).start(priority=1)
+
+    @pl.loop(1, PAIRS - 1)
     def _(i):
         k_copy(i).wait()
         v_copy(i - 1).wait()
@@ -181,11 +184,11 @@
 
         @pl.when(i + DEPTH < PAIRS)
         def _():
-            k_copy(i + DEPTH).start()
+            k_copy(i + DEPTH).start(priority=1)
 
         @pl.when(i - 1 + DEPTH < PAIRS)
         def _():
-            v_copy(i - 1 + DEPTH).start()
+            v_copy(i - 1 + DEPTH).start(priority=1)
 
         @pl.when(i == 3)
         def _():
@@ -195,13 +198,8 @@
 
         @pl.when((n >= 0) & (n < PIECES))
         def _():
-            wm_copy(wg_hbm, n, n).start()
-            wm_copy(wu_hbm, n, PIECES + n).start()
-
-        @pl.when(n == PIECES)
-        def _():
-            wm_copy(wd_hbm, 0, 2 * PIECES).start()
-            wm_copy(wd_hbm, 1, 2 * PIECES + 1).start()
+            wm_copy(wg_hbm, n, n).start(priority=1)
+            wm_copy(wu_hbm, n, PIECES + n).start(priority=1)
 
         j = i // PER - 1
         step = lax.rem(i, PER)
@@ -224,68 +222,98 @@
         def _():
             finish(j - 1)
 
-    wm_copy(wd_hbm, 2, 2 * PIECES + 2).start()
-    wm_copy(wd_hbm, 3, 2 * PIECES + 3).start()
+    wm_copy(wd_hbm, 0, 2 * PIECES).start(priority=1)
+    wm_copy(wd_hbm, 1, 2 * PIECES + 1).start(priority=1)
+    k_copy(PAIRS - 1).wait()
     w = weights(s_s[...])
+    s_s[...] = scores(PAIRS - 1)
+    wm_copy(wd_hbm, 2, 2 * PIECES + 2).start(priority=1)
+    v_copy(PAIRS - 2).wait()
+    o_s[PAIRS - 2] = values(PAIRS - 2, w)
+    w = weights(s_s[...])
+    wm_copy(wd_hbm, 3, 2 * PIECES + 3).start(priority=1)
     v_copy(PAIRS - 1).wait()
     o_s[PAIRS - 1] = values(PAIRS - 1, w)
     last = CHUNKS - 1
     project(last)
     for n in range(3):
         direct(n).start()
+
+    def normed_rows(rows):
+        h = [hb[s, rows].astype(F32).reshape(-1, HALF) for s in range(2)]
+        blocks = [h[j // 8][:, (j % 8) * 128 : (j % 8 + 1) * 128] for j in range(D // 128)]
+        return jnp.concatenate(normed(blocks, gm[...].astype(F32)), 1)
+
+    finish(last - 2)
     finish(last - 1)
     for j in range(last):
         first_c(j).wait()
+    done = normed_rows(slice(0, last))
+    act[0 : last * CHUNK] = done
     for n in range(3):
         direct(n).wait()
     for s in range(2):
         near = t1[last, s].astype(F32) + d1[0, s].astype(F32)
         far = d1[1, s].astype(F32) + d1[2, s].astype(F32)
         hb[s, last] = (xb[last, :, s * HALF : (s + 1) * HALF].astype(F32) + (near + far)).astype(BF16)
-
-    h = [hb[s].astype(F32).reshape(ROWS, HALF) for s in range(2)]
-    blocks = [h[j // 8][:, (j % 8) * 128 : (j % 8 + 1) * 128] for j in range(D // 128)]
-    for j, b in enumerate(normed(blocks, gm[...].astype(F32))):
-        act[:, j * 128 : (j + 1) * 128] = b
-
-    for n in range(PIECES):
-        wm_copy(wg_hbm, n, n).wait()
-        wm_copy(wu_hbm, n, PIECES + n).wait()
+    act[last * CHUNK :] = normed_rows(slice(last, CHUNKS))
+
+    def hidden(n):
+        cols = slice(n % 2 * 256, n % 2 * 256 + 256)
+        return dot(act[...], wm[n // 2, :, cols]), dot(act[...], wm[PIECES + n // 2, :, cols])
+
+    def keep(n, gate, up):
+        hid[:, n * 256 : (n + 1) * 256] = (gate * (1.0 / (1.0 + jnp.exp(-gate))) * up).astype(BF16)
+
+    late = None
     for n in range(FF // 256):
-        cols = slice(n % 2 * 256, n % 2 * 256 + 256)
-        gate = dot(act[...], wm[n // 2, :, cols])
-        up = dot(act[...], wm[PIECES + n // 2, :, cols])
-        hid[:, n * 256 : (n + 1) * 256] = (gate * (1.0 / (1.0 + jnp.exp(-gate))) * up).astype(BF16)
-
-    def second_a(n):
-        return send(t2.at[n, other], r2.at[n], s2.at[0], n, mate)
-
-    def second_b(n):
-        return send(a2.at[n], b2.at[n], s2.at[1], n, across)
-
-    def cols_of(n):
-        return pl.ds(pl.multiple_of(n * NCOL + core * (NCOL // 2), NCOL // 2), NCOL // 2)
-
-    def second_c(n):
-        return send(y.at[:, cols_of(n)], y.at[:, cols_of(n)], s2.at[2], n, mate)
-
-    for n in range(PIECES):
-        wm_copy(wd_hbm, n, 2 * PIECES + n).wait()
-        for s in range(2):
-            t2[n, s] = dot(hid[...], wm[2 * PIECES + n, :, s * (NCOL // 2) : (s + 1) * (NCOL // 2)]).astype(BF16)
-        second_a(n).start()
-    for n in range(PIECES):
-        second_a(n).wait()
-        a2[n] = (t2[n, core].astype(F32) + r2[n].astype(F32)).astype(BF16)
-        second_b(n).start()
-    for n in range(PIECES):
-        second_b(n).wait()
-        off = pl.multiple_of(n % 2 * NCOL + core * (NCOL // 2), NCOL // 2)
-        mine = hb[n // 2, :, :, pl.ds(off, NCOL // 2)].astype(F32).reshape(ROWS, NCOL // 2)
-        y[:, cols_of(n)] = (mine + (a2[n].astype(F32) + b2[n].astype(F32))).astype(BF16)
-        second_c(n).start()
-    for n in range(PIECES):
-        second_c(n).wait()
+        for m in {0: range(PIECES - 1), FF // 256 - 2: range(PIECES - 1, PIECES)}.get(n, ()):
+            wm_copy(wg_hbm, m, m).wait()
+            wm_copy(wu_hbm, m, PIECES + m).wait()
+        pair = hidden(n)
+        if late is not None:
+            keep(n - 1, *late)
+        late = pair
+    keep(FF // 256 - 1, *late)
+
+    def second_a(u):
+        return send(t2.at[u], r2.at[u], s2.at[0], u, mate)
+
+    def second_b(u):
+        return send(a2.at[u], b2.at[u], s2.at[1], u, across)
+
+    def cols_of(u):
+        return pl.ds(pl.multiple_of(core * HALF + u * SUB, SUB), SUB)
+
+    def second_c(u):
+        return send(y.at[:, cols_of(u)], y.at[:, cols_of(u)], s2.at[2], u, mate)
+
+    def down(half, u):
+        n = half * 2 + u * SUB // NCOL
+        if u * SUB % NCOL == 0:
+            wm_copy(wd_hbm, n, 2 * PIECES + n).wait()
+        return dot(hid[...], wm[2 * PIECES + n, :, u * SUB % NCOL : u * SUB % NCOL + SUB])
+
+    ahead = down(0, 0)
+    for u in range(SUBS):
+        t = ahead
+        if u + 1 < SUBS:
+            ahead = down(0, u + 1)
+        t2[u] = t.astype(BF16)
+        second_a(u).start()
+    for first in range(0, SUBS, 2):
+        terms = [down(1, u) for u in range(first, first + 2)]
+        for u, t in enumerate(terms, first):
+            second_a(u).wait()
+            a2[u] = (t + r2[u].astype(F32)).astype(BF16)
+            second_b(u).start()
+    for u in range(SUBS):
+        second_b(u).wait()
+        mine = hb[core, :, :, u * SUB : (u + 1) * SUB].astype(F32).reshape(ROWS, SUB)
+        y[:, cols_of(u)] = (mine + (a2[u].astype(F32) + b2[u].astype(F32))).astype(BF16)
+        second_c(u).start()
+    for u in range(SUBS):
+        second_c(u).wait()
 
 
 def layer(x, k_cache, v_cache, gain_a, wq, wo, gain_m, w_gate, w_up, w_down):
@@ -317,17 +345,17 @@
             vmem((CHUNKS, CHUNK, HALF), BF16),
             vmem((2, CHUNKS, CHUNK, HALF), BF16),
             vmem((3, 2, CHUNK, HALF), BF16),
-            vmem((PIECES, 2, ROWS, NCOL // 2), BF16),
-            vmem((PIECES, ROWS, NCOL // 2), BF16),
-            vmem((PIECES, ROWS, NCOL // 2), BF16),
-            vmem((PIECES, ROWS, NCOL // 2), BF16),
+            vmem((SUBS, ROWS, SUB), BF16),
+            vmem((SUBS, ROWS, SUB), BF16),
+            vmem((SUBS, ROWS, SUB), BF16),
+            vmem((SUBS, ROWS, SUB), BF16),
             dma((6,)),
             dma((DEPTH,)),
             dma((DEPTH,)),
             dma((3 * PIECES,)),
             dma((3, 2, CHUNKS)),
             dma((2, 3)),
-            dma((3, 2, PIECES)),
+            dma((3, 2, SUBS)),
         ],
         compiler_params=pltpu.CompilerParams(collective_id=0, has_side_effects=True, vmem_limit_bytes=62000000),
     )(

time: 61.6 us -> 59.5 us (0.966)
  Pallas kernels: 60.8 us -> 58.7 us
    pallas_call x1, Pallas kernels: 60.8 us -> 58.7 us  [layer(): pl.pallas_call(kernel, out_shape=pltpu.VMEM((ROWS, D), BF16), in_specs=[h...]
where the time goes in v3:
time: 59.5 us
  Pallas kernels  58.7 us (99%)
  local copies, waits for them, and re-layouts  0.71 us (1%)
    pallas_call x1, Pallas kernels, layer(): pl.pallas_call(kernel, out_shape=pltpu.VMEM((ROWS, D), BF16), in_specs=[h...  58.7 us

profile of v3, /device:TPU:0, one launch (start us, length us, event | category | flops | bytes accessed | tf_op | source)
XLA Modules:
  0.0 59.5 jit_solution(18219857387103238414)
XLA Ops:
  0.0 58.7 %shard_map.109 = bf16[64,2048]{1,0:T(8,128)(2,1)S(1)} custom-call(bf16[8,8,2048]{2,1,0:T(8,128)(2,1)} %bitcast.5, bf16[8,2,4,4096,128]{4,3,2,1,0:T(8,128)(2,1)} %bitcast.1.k_hbm, bf16[8,2,4,4096,128]{4,3,2,1,0:T(8,128)(2,1)} %bitcast.2.v_hbm, bf16[16,128]{1,0:T(8,128)(2,1)} %bitcast.6, bf16[2048,512]{1,0:T(8,128)(2,1)} %wq_hbm.1, bf16[512,2048]{1,0:T(8,128)(2,1)} %wo_hbm.1, ...), custom_call_target="tpu_custom_call" | custom-call | tf_op jit(solution)/shard_map/pallas_call | solution.py:322
  58.8 0.7 %copy.13 = bf16[64,2048]{1,0:T(8,128)(2,1)} copy(bf16[64,2048]{1,0:T(8,128)(2,1)S(1)} %shard_map.109) | data formatting | bytes 524288

commit v4 on v3

--- a/solution.py
+++ b/solution.py
@@ -18,10 +18,10 @@
 PER = CHUNK // 2
 HALF = D // 2
 FF = 2048
+TALL = 128
 NCOL = 512
 PIECES = D // NCOL
-SUB = 256
-SUBS = HALF // SUB
+SUB = NCOL // 2
 F32, BF16 = jnp.float32, jnp.bfloat16
 
 
@@ -50,7 +50,7 @@
 def kernel(
     x_hbm, k_hbm, v_hbm, ga_hbm, wq_hbm, wo_hbm, gm_hbm, wg_hbm, wu_hbm, wd_hbm, rope_hbm, y,
     xb, ga, gm, rope, wq, wo, wm, kbuf, vbuf, q_s, s_s, o_s, act, hid,
-    t1, r1, a1, b1, hb, d1, t2, r2, a2, b2,
+    t1, r1, a1, b1, hb, d1, t2, t3, r2, a2, b2,
     in_sem, k_sem, v_sem, wm_sem, s1, sd, s2,
 ):
     tp = lax.axis_index("tp")
@@ -58,11 +58,13 @@
     chip = tp // 2
     other = 1 - core
     mate = {"tp": chip * 2 + other}
-    across = {"tp": (1 - chip) * 2 + core}
     corner = {"tp": (1 - chip) * 2 + other}
+    far = [{"tp": (1 - chip) * 2 + c} for c in range(2)]
+    own = lax.rem(core + chip, 2)
+    theirs = 1 - own
 
     barrier = pltpu.get_barrier_semaphore()
-    for device in (mate, across, corner):
+    for device in (mate, *far):
         pl.semaphore_signal(barrier, inc=1, device_id=device, device_id_type=MESH)
 
     def k_copy(i):
@@ -74,8 +76,7 @@
         return pltpu.make_async_copy(v_hbm.at[i // PER, :, lax.rem(i, PER)], vbuf.at[slot], v_sem.at[slot])
 
     def wm_copy(w_hbm, n, piece):
-        start = n * NCOL if w_hbm is not wd_hbm else lax.rem(n // 2 + other, 2) * HALF + n % 2 * NCOL
-        cols = pl.ds(pl.multiple_of(start, NCOL), NCOL)
+        cols = pl.ds(pl.multiple_of(n * NCOL, NCOL), NCOL)
         return pltpu.make_async_copy(w_hbm.at[:, cols], wm.at[piece], wm_sem.at[piece])
 
     firsts = [
@@ -95,8 +96,10 @@
         c.wait()
     blocks = [xb[:, :, j * 128 : (j + 1) * 128].astype(F32).reshape(ROWS, 128) for j in range(D // 128)]
     for j, b in enumerate(normed(blocks, ga[...].astype(F32))):
-        act[:, j * 128 : (j + 1) * 128] = b
-    q = dot(act[...], wq[...]).astype(BF16).astype(F32)
+        act[0:ROWS, j * 128 : (j + 1) * 128] = b
+    act[ROWS:] = jnp.zeros((TALL - ROWS, D), BF16)
+    hid[ROWS:] = jnp.zeros((TALL - ROWS, FF), BF16)
+    q = dot(act[0:ROWS], wq[...]).astype(BF16).astype(F32)
     cos, sin = rope[0:1, :], rope[1:2, :]
     for h in range(HEADS):
         t = q[:, h * HEAD : (h + 1) * HEAD]
@@ -136,16 +139,30 @@
         )
 
     def first_a(j):
-        return send(t1.at[j, other], r1.at[j], s1.at[0], j, mate)
+        return send(t1.at[j, theirs], r1.at[j], s1.at[0], j, mate)
 
     def first_b(j):
-        return send(a1.at[j], b1.at[j], s1.at[1], j, across)
+        return send(a1.at[j], b1.at[j], s1.at[1], j, corner)
 
     def first_c(j):
-        return send(hb.at[core, j], hb.at[core, j], s1.at[2], j, mate)
+        return send(hb.at[own, j], hb.at[own, j], s1.at[2], j, mate)
 
     def direct(n):
-        return send(t1.at[CHUNKS - 1], d1.at[n], sd, n, (mate, across, corner)[n])
+        return pltpu.make_async_remote_copy(
+            src_ref=t1.at[CHUNKS - 1],
+            dst_ref=d1.at[core if n < 2 else 2],
+            send_sem=sd.at[0, n],
+            recv_sem=sd.at[1, core if n < 2 else 2],
+            device_id=(*far, mate)[n],
+            device_id_type=MESH,
+        )
+
+    def direct_done():
+        for n in range(3):
+            direct(n).wait_send()
+            pltpu.make_async_remote_copy(
+                src_ref=t1.at[CHUNKS - 1], dst_ref=d1.at[n], send_sem=sd.at[0, n], recv_sem=sd.at[1, n], device_id=mate, device_id_type=MESH
+            ).wait_recv()
 
     def project(j):
         o = jnp.concatenate(
@@ -160,13 +177,13 @@
 
     def fold(j):
         first_a(j).wait()
-        a1[j] = (t1[j, core].astype(F32) + r1[j].astype(F32)).astype(BF16)
+        a1[j] = (t1[j, own].astype(F32) + r1[j].astype(F32)).astype(BF16)
         first_b(j).start()
 
     def finish(j):
         first_b(j).wait()
-        mine = xb[j, :, pl.ds(pl.multiple_of(core * HALF, HALF), HALF)].astype(F32)
-        hb[core, j] = (mine + (a1[j].astype(F32) + b1[j].astype(F32))).astype(BF16)
+        mine = xb[j, :, pl.ds(pl.multiple_of(own * HALF, HALF), HALF)].astype(F32)
+        hb[own, j] = (mine + (a1[j].astype(F32) + b1[j].astype(F32))).astype(BF16)
         first_c(j).start()
 
     k_copy(0).wait()
@@ -250,24 +267,23 @@
         first_c(j).wait()
     done = normed_rows(slice(0, last))
     act[0 : last * CHUNK] = done
-    for n in range(3):
-        direct(n).wait()
+    direct_done()
     for s in range(2):
-        near = t1[last, s].astype(F32) + d1[0, s].astype(F32)
-        far = d1[1, s].astype(F32) + d1[2, s].astype(F32)
-        hb[s, last] = (xb[last, :, s * HALF : (s + 1) * HALF].astype(F32) + (near + far)).astype(BF16)
-    act[last * CHUNK :] = normed_rows(slice(last, CHUNKS))
+        here = t1[last, s].astype(F32) + d1[2, s].astype(F32)
+        there = d1[0, s].astype(F32) + d1[1, s].astype(F32)
+        hb[s, last] = (xb[last, :, s * HALF : (s + 1) * HALF].astype(F32) + (here + there)).astype(BF16)
+    act[last * CHUNK : ROWS] = normed_rows(slice(last, CHUNKS))
 
     def hidden(n):
         cols = slice(n % 2 * 256, n % 2 * 256 + 256)
-        return dot(act[...], wm[n // 2, :, cols]), dot(act[...], wm[PIECES + n // 2, :, cols])
+        return dot(act[...], wm[n // 2, :, cols])[:ROWS], dot(act[...], wm[PIECES + n // 2, :, cols])[:ROWS]
 
     def keep(n, gate, up):
-        hid[:, n * 256 : (n + 1) * 256] = (gate * (1.0 / (1.0 + jnp.exp(-gate))) * up).astype(BF16)
+        hid[0:ROWS, n * 256 : (n + 1) * 256] = (gate * (1.0 / (1.0 + jnp.exp(-gate))) * up).astype(BF16)
 
     late = None
     for n in range(FF // 256):
-        for m in {0: range(PIECES - 1), FF // 256 - 2: range(PIECES - 1, PIECES)}.get(n, ()):
+        for m in {0: (0, 1), 4: (2,), 6: (3,)}.get(n, ()):
             wm_copy(wg_hbm, m, m).wait()
             wm_copy(wu_hbm, m, PIECES + m).wait()
         pair = hidden(n)
@@ -276,44 +292,42 @@
         late = pair
     keep(FF // 256 - 1, *late)
 
-    def second_a(u):
-        return send(t2.at[u], r2.at[u], s2.at[0], u, mate)
-
-    def second_b(u):
-        return send(a2.at[u], b2.at[u], s2.at[1], u, across)
-
-    def cols_of(u):
-        return pl.ds(pl.multiple_of(core * HALF + u * SUB, SUB), SUB)
-
-    def second_c(u):
-        return send(y.at[:, cols_of(u)], y.at[:, cols_of(u)], s2.at[2], u, mate)
-
-    def down(half, u):
-        n = half * 2 + u * SUB // NCOL
-        if u * SUB % NCOL == 0:
-            wm_copy(wd_hbm, n, 2 * PIECES + n).wait()
-        return dot(hid[...], wm[2 * PIECES + n, :, u * SUB % NCOL : u * SUB % NCOL + SUB])
-
-    ahead = down(0, 0)
-    for u in range(SUBS):
-        t = ahead
-        if u + 1 < SUBS:
-            ahead = down(0, u + 1)
-        t2[u] = t.astype(BF16)
-        second_a(u).start()
-    for first in range(0, SUBS, 2):
-        terms = [down(1, u) for u in range(first, first + 2)]
-        for u, t in enumerate(terms, first):
-            second_a(u).wait()
-            a2[u] = (t + r2[u].astype(F32)).astype(BF16)
-            second_b(u).start()
-    for u in range(SUBS):
-        second_b(u).wait()
-        mine = hb[core, :, :, u * SUB : (u + 1) * SUB].astype(F32).reshape(ROWS, SUB)
-        y[:, cols_of(u)] = (mine + (a2[u].astype(F32) + b2[u].astype(F32))).astype(BF16)
-        second_c(u).start()
-    for u in range(SUBS):
-        second_c(u).wait()
+    def second_a(n):
+        return send(t2.at[n], r2.at[n], s2.at[0], n, mate)
+
+    def second_b(n):
+        return send(a2.at[n], b2.at[n], s2.at[1], n, corner)
+
+    def cols_of(n):
+        return pl.ds(pl.multiple_of(n * NCOL + own * SUB, SUB), SUB)
+
+    def second_c(n):
+        return send(y.at[:, cols_of(n)], y.at[:, cols_of(n)], s2.at[2], n, mate)
+
+    def down(n):
+        wm_copy(wd_hbm, n, 2 * PIECES + n).wait()
+        t2[n] = dot(hid[...], wm[2 * PIECES + n, :, pl.ds(pl.multiple_of(theirs * SUB, SUB), SUB)])[:ROWS].astype(BF16)
+        t3[n] = dot(hid[...], wm[2 * PIECES + n, :, pl.ds(pl.multiple_of(own * SUB, SUB), SUB)])[:ROWS]
+        second_a(n).start()
+
+    def cross(n):
+        second_a(n).wait()
+        a2[n] = (t3[n] + r2[n].astype(F32)).astype(BF16)
+        second_b(n).start()
+
+    for n in range(PIECES):
+        down(n)
+        if n >= 1:
+            cross(n - 1)
+    cross(PIECES - 1)
+    for n in range(PIECES):
+        second_b(n).wait()
+        off = pl.multiple_of(n % 2 * NCOL + own * SUB, SUB)
+        mine = hb[n // 2, :, :, pl.ds(off, SUB)].astype(F32).reshape(ROWS, SUB)
+        y[:, cols_of(n)] = (mine + (a2[n].astype(F32) + b2[n].astype(F32))).astype(BF16)
+        second_c(n).start()
+    for n in range(PIECES):
+        second_c(n).wait()
 
 
 def layer(x, k_cache, v_cache, gain_a, wq, wo, gain_m, w_gate, w_up, w_down):
@@ -337,25 +351,26 @@
             vmem((ROWS, HEADS * HEAD), F32),
             vmem((8, KV), F32),
             vmem((PAIRS, 8, 2 * HEAD), F32),
-            vmem((ROWS, D), BF16),
-            vmem((ROWS, FF), BF16),
+            vmem((TALL, D), BF16),
+            vmem((TALL, FF), BF16),
             vmem((CHUNKS, 2, CHUNK, HALF), BF16),
             vmem((CHUNKS, CHUNK, HALF), BF16),
             vmem((CHUNKS, CHUNK, HALF), BF16),
             vmem((CHUNKS, CHUNK, HALF), BF16),
             vmem((2, CHUNKS, CHUNK, HALF), BF16),
             vmem((3, 2, CHUNK, HALF), BF16),
-            vmem((SUBS, ROWS, SUB), BF16),
-            vmem((SUBS, ROWS, SUB), BF16),
-            vmem((SUBS, ROWS, SUB), BF16),
-            vmem((SUBS, ROWS, SUB), BF16),
+            vmem((PIECES, ROWS, SUB), BF16),
+            vmem((PIECES, ROWS, SUB), F32),
+            vmem((PIECES, ROWS, SUB), BF16),
+            vmem((PIECES, ROWS, SUB), BF16),
+            vmem((PIECES, ROWS, SUB), BF16),
             dma((6,)),
             dma((DEPTH,)),
             dma((DEPTH,)),
             dma((3 * PIECES,)),
             dma((3, 2, CHUNKS)),
             dma((2, 3)),
-            dma((3, 2, SUBS)),
+            dma((3, 2, PIECES)),
         ],
         compiler_params=pltpu.CompilerParams(collective_id=0, has_side_effects=True, vmem_limit_bytes=62000000),
     )(

time: 59.5 us -> 58.2 us (0.978)
  Pallas kernels: 58.7 us -> 57.4 us
    pallas_call x1, Pallas kernels: 58.7 us -> 57.4 us  [layer(): pl.pallas_call(kernel, out_shape=pltpu.VMEM((ROWS, D), BF16), in_specs=[h...]
where the time goes in v4:
time: 58.2 us; the launch traced here: 58.1 us
  Pallas kernels  57.4 us (99%)
  local copies, waits for them, and re-layouts  0.71 us (1%)
    pallas_call x1, Pallas kernels, layer(): pl.pallas_call(kernel, out_shape=pltpu.VMEM((ROWS, D), BF16), in_specs=[h...  57.4 us

profile of v4, /device:TPU:0, one launch (start us, length us, event | category | flops | bytes accessed | tf_op | source)
XLA Modules:
  0.0 58.1 jit_solution(16544784364491779158)
XLA Ops:
  0.0 57.4 %shard_map.109 = bf16[64,2048]{1,0:T(8,128)(2,1)S(1)} custom-call(bf16[8,8,2048]{2,1,0:T(8,128)(2,1)} %bitcast.5, bf16[8,2,4,4096,128]{4,3,2,1,0:T(8,128)(2,1)} %bitcast.1.k_hbm, bf16[8,2,4,4096,128]{4,3,2,1,0:T(8,128)(2,1)} %bitcast.2.v_hbm, bf16[16,128]{1,0:T(8,128)(2,1)} %bitcast.6, bf16[2048,512]{1,0:T(8,128)(2,1)} %wq_hbm.1, bf16[512,2048]{1,0:T(8,128)(2,1)} %wo_hbm.1, ...), custom_call_target="tpu_custom_call" | custom-call | tf_op jit(solution)/shard_map/pallas_call | solution.py:336
  57.4 0.7 %copy.13 = bf16[64,2048]{1,0:T(8,128)(2,1)} copy(bf16[64,2048]{1,0:T(8,128)(2,1)S(1)} %shard_map.109) | data formatting | bytes 524288

commit v5 on v4

--- a/solution.py
+++ b/solution.py
@@ -50,8 +50,8 @@
 def kernel(
     x_hbm, k_hbm, v_hbm, ga_hbm, wq_hbm, wo_hbm, gm_hbm, wg_hbm, wu_hbm, wd_hbm, rope_hbm, y,
     xb, ga, gm, rope, wq, wo, wm, kbuf, vbuf, q_s, s_s, o_s, act, hid,
-    t1, r1, a1, b1, hb, d1, t2, t3, r2, a2, b2,
-    in_sem, k_sem, v_sem, wm_sem, s1, sd, s2,
+    t1, hb, d1, actf, t2, t3, r2, a2, b2,
+    in_sem, k_sem, v_sem, wm_sem, sd, s2,
 ):
     tp = lax.axis_index("tp")
     core = lax.rem(tp, 2)
@@ -138,31 +138,35 @@
             src_ref=src, dst_ref=dst, send_sem=sems.at[0, n], recv_sem=sems.at[1, n], device_id=device, device_id_type=MESH
         )
 
-    def first_a(j):
-        return send(t1.at[j, theirs], r1.at[j], s1.at[0], j, mate)
-
-    def first_b(j):
-        return send(a1.at[j], b1.at[j], s1.at[1], j, corner)
-
-    def first_c(j):
-        return send(hb.at[own, j], hb.at[own, j], s1.at[2], j, mate)
-
-    def direct(n):
+    def direct(j, n):
+        slot = core if n < 2 else 2
         return pltpu.make_async_remote_copy(
-            src_ref=t1.at[CHUNKS - 1],
-            dst_ref=d1.at[core if n < 2 else 2],
-            send_sem=sd.at[0, n],
-            recv_sem=sd.at[1, core if n < 2 else 2],
+            src_ref=t1.at[j],
+            dst_ref=d1.at[j, slot],
+            send_sem=sd.at[0, n, j],
+            recv_sem=sd.at[1, slot, j],
             device_id=(*far, mate)[n],
             device_id_type=MESH,
         )
 
-    def direct_done():
+    def landed(j, n):
+        return pltpu.make_async_remote_copy(
+            src_ref=t1.at[j], dst_ref=d1.at[j, n], send_sem=sd.at[0, n, j], recv_sem=sd.at[1, n, j], device_id=mate, device_id_type=MESH
+        )
+
+    def take(j):
         for n in range(3):
-            direct(n).wait_send()
-            pltpu.make_async_remote_copy(
-                src_ref=t1.at[CHUNKS - 1], dst_ref=d1.at[n], send_sem=sd.at[0, n], recv_sem=sd.at[1, n], device_id=mate, device_id_type=MESH
-            ).wait_recv()
+            landed(j, n).wait()
+        parts = []
+        for s in range(2):
+            here = t1[j, s].astype(F32) + d1[j, 2, s].astype(F32)
+            there = d1[j, 0, s].astype(F32) + d1[j, 1, s].astype(F32)
+            h = (xb[j, :, s * HALF : (s + 1) * HALF].astype(F32) + (here + there)).astype(BF16)
+            hb[s, j] = h
+            h = h.astype(F32)
+            parts += [h[:, k * 128 : (k + 1) * 128] for k in range(HALF // 128)]
+        for k, b in enumerate(normed(parts, gm[...].astype(F32))):
+            actf[j, :, k * 128 : (k + 1) * 128] = b.astype(F32)
 
     def project(j):
         o = jnp.concatenate(
@@ -175,17 +179,6 @@
         for s in range(2):
             t1[j, s] = dot(o, wo[:, s * HALF : (s + 1) * HALF]).astype(BF16)
 
-    def fold(j):
-        first_a(j).wait()
-        a1[j] = (t1[j, own].astype(F32) + r1[j].astype(F32)).astype(BF16)
-        first_b(j).start()
-
-    def finish(j):
-        first_b(j).wait()
-        mine = xb[j, :, pl.ds(pl.multiple_of(own * HALF, HALF), HALF)].astype(F32)
-        hb[own, j] = (mine + (a1[j].astype(F32) + b1[j].astype(F32))).astype(BF16)
-        first_c(j).start()
-
     k_copy(0).wait()
     s_s[...] = scores(0)
     k_copy(DEPTH).start(priority=1)
@@ -229,15 +222,12 @@
         @pl.when((i >= PER) & (step == 0))
         def _():
             project(j)
-            first_a(j).start()
-
-        @pl.when((i >= PER) & (step == 2))
-        def _():
-            fold(j)
+            for n in range(3):
+                direct(j, n).start()
 
         @pl.when((i >= 2 * PER) & (step == 3))
         def _():
-            finish(j - 1)
+            take(j - 1)
 
     wm_copy(wd_hbm, 0, 2 * PIECES).start(priority=1)
     wm_copy(wd_hbm, 1, 2 * PIECES + 1).start(priority=1)
@@ -254,25 +244,11 @@
     last = CHUNKS - 1
     project(last)
     for n in range(3):
-        direct(n).start()
-
-    def normed_rows(rows):
-        h = [hb[s, rows].astype(F32).reshape(-1, HALF) for s in range(2)]
-        blocks = [h[j // 8][:, (j % 8) * 128 : (j % 8 + 1) * 128] for j in range(D // 128)]
-        return jnp.concatenate(normed(blocks, gm[...].astype(F32)), 1)
-
-    finish(last - 2)
-    finish(last - 1)
-    for j in range(last):
-        first_c(j).wait()
-    done = normed_rows(slice(0, last))
-    act[0 : last * CHUNK] = done
-    direct_done()
-    for s in range(2):
-        here = t1[last, s].astype(F32) + d1[2, s].astype(F32)
-        there = d1[0, s].astype(F32) + d1[1, s].astype(F32)
-        hb[s, last] = (xb[last, :, s * HALF : (s + 1) * HALF].astype(F32) + (here + there)).astype(BF16)
-    act[last * CHUNK : ROWS] = normed_rows(slice(last, CHUNKS))
+        direct(last, n).start()
+    take(last - 2)
+    take(last - 1)
+    take(last)
+    act[0:ROWS] = actf[...].reshape(ROWS, D).astype(BF16)
 
     def hidden(n):
         cols = slice(n % 2 * 256, n % 2 * 256 + 256)
@@ -311,7 +287,7 @@
         second_a(n).start()
 
     def cross(n):
-        second_a(n).wait()
+        second_a(n).wait_recv()
         a2[n] = (t3[n] + r2[n].astype(F32)).astype(BF16)
         second_b(n).start()
 
@@ -321,13 +297,15 @@
             cross(n - 1)
     cross(PIECES - 1)
     for n in range(PIECES):
-        second_b(n).wait()
+        second_b(n).wait_recv()
         off = pl.multiple_of(n % 2 * NCOL + own * SUB, SUB)
         mine = hb[n // 2, :, :, pl.ds(off, SUB)].astype(F32).reshape(ROWS, SUB)
         y[:, cols_of(n)] = (mine + (a2[n].astype(F32) + b2[n].astype(F32))).astype(BF16)
         second_c(n).start()
     for n in range(PIECES):
         second_c(n).wait()
+        second_a(n).wait_send()
+        second_b(n).wait_send()
 
 
 def layer(x, k_cache, v_cache, gain_a, wq, wo, gain_m, w_gate, w_up, w_down):
@@ -354,11 +332,9 @@
             vmem((TALL, D), BF16),
             vmem((TALL, FF), BF16),
             vmem((CHUNKS, 2, CHUNK, HALF), BF16),
-            vmem((CHUNKS, CHUNK, HALF), BF16),
-            vmem((CHUNKS, CHUNK, HALF), BF16),
-            vmem((CHUNKS, CHUNK, HALF), BF16),
             vmem((2, CHUNKS, CHUNK, HALF), BF16),
-            vmem((3, 2, CHUNK, HALF), BF16),
+            vmem((CHUNKS, 3, 2, CHUNK, HALF), BF16),
+            vmem((CHUNKS, CHUNK, D), F32),
             vmem((PIECES, ROWS, SUB), BF16),
             vmem((PIECES, ROWS, SUB), F32),
             vmem((PIECES, ROWS, SUB), BF16),
@@ -368,8 +344,7 @@
             dma((DEPTH,)),
             dma((DEPTH,)),
             dma((3 * PIECES,)),
-            dma((3, 2, CHUNKS)),
-            dma((2, 3)),
+            dma((2, 3, CHUNKS)),
             dma((3, 2, PIECES)),
         ],
         compiler_params=pltpu.CompilerParams(collective_id=0, has_side_effects=True, vmem_limit_bytes=62000000),

time: 58.2 us -> 58.1 us (level)
  no operation moved by 1% of the time
where the time goes in v5:
time: 58.1 us; the launch traced here: 58 us
  Pallas kernels  57.3 us (99%)
  local copies, waits for them, and re-layouts  0.71 us (1%)
    pallas_call x1, Pallas kernels, layer(): pl.pallas_call(kernel, out_shape=pltpu.VMEM((ROWS, D), BF16), in_specs=[h...  57.3 us

profile of v5, /device:TPU:0, one launch (start us, length us, event | category | flops | bytes accessed | tf_op | source)
XLA Modules:
  0.0 58.0 jit_solution(16917594429208088995)
XLA Ops:
  0.0 57.3 %shard_map.109 = bf16[64,2048]{1,0:T(8,128)(2,1)S(1)} custom-call(bf16[8,8,2048]{2,1,0:T(8,128)(2,1)} %bitcast.5, bf16[8,2,4,4096,128]{4,3,2,1,0:T(8,128)(2,1)} %bitcast.1.k_hbm, bf16[8,2,4,4096,128]{4,3,2,1,0:T(8,128)(2,1)} %bitcast.2.v_hbm, bf16[16,128]{1,0:T(8,128)(2,1)} %bitcast.6, bf16[2048,512]{1,0:T(8,128)(2,1)} %wq_hbm.1, bf16[512,2048]{1,0:T(8,128)(2,1)} %wo_hbm.1, ...), custom_call_target="tpu_custom_call" | custom-call | tf_op jit(solution)/shard_map/pallas_call | solution.py:314
  57.3 0.7 %copy.13 = bf16[64,2048]{1,0:T(8,128)(2,1)} copy(bf16[64,2048]{1,0:T(8,128)(2,1)S(1)} %shard_map.109) | data formatting | bytes 524288
